TPU v7x, 32 devices: a whole 2x2x4 slice. The times are simulated.
32 devices in a mesh: dp: 1, tp: 32 (over x, y, z, core).
Axes of the slice: x: 2, y: 2, z: 4, core: 2. Of those that a mesh axis runs over, the one named last changes fastest.
Arguments:
- x: bfloat16 [2048, 4608], P('dp')
- w_gate: bfloat16 [4608, 36864], P(None, 'tp')
- w_up: bfloat16 [4608, 36864], P(None, 'tp')
- w_down: bfloat16 [36864, 4608], P('tp')
Outputs:
- output: bfloat16 [2048, 4608], P('dp')
All inputs are finite; a program needn't handle non-finite values.
Results may differ from a plain program's by a relative error of at most 0.016.
Values are sent between devices in bfloat16 or wider.
A program may use at most 2 GiB of HBM per device.

v0:
```python
import jax
import jax.numpy as jnp
from jax import lax
from jax.sharding import PartitionSpec as P


def solution(mesh):
    def step(x, w_gate, w_up, w_down):
        gate = jnp.dot(x, w_gate, preferred_element_type=jnp.float32)
        up = jnp.dot(x, w_up, preferred_element_type=jnp.float32)
        hidden = (jax.nn.gelu(gate) * up).astype(jnp.bfloat16)
        term = jnp.dot(hidden, w_down, preferred_element_type=jnp.float32).astype(jnp.bfloat16)
        return lax.psum(term, "tp")

    return jax.shard_map(
        step,
        mesh=mesh,
        in_specs=(P("dp", None), P(None, "tp"), P(None, "tp"), P("tp", None)),
        out_specs=P("dp", None),
        check_vma=False,
    )
```

profile of v0, /device:TPU:0, one launch (start us, length us, event | category | flops | bytes accessed | tf_op | source)
XLA Modules:
  0.0 430.8 jit_solution(16394620991039073033)
XLA Ops:
  6.5 0.0 all-reduce.2.cloned.1.call-start
  6.5 0.0 copy-start
  6.5 32.0 %fusion.8 = f32[2048,1152]{1,0:T(8,128)} fusion(bf16[2048,4608]{1,0:T(8,128)(2,1)} %param.4, bf16[4608,1152]{1,0:T(8,128)(2,1)} %param.5), kind=kOutput, calls=%fused_computation.11 | convolution fusion | flops 21743271936 | bytes 38928384 | tf_op jit(solution)/shard_map/dot_general | solution.py:9
  38.5 0.0 copy-done
  38.5 32.4 %fusion.7 = bf16[2048,1152]{1,0:T(8,128)(2,1)S(1)} fusion(bf16[2048,4608]{1,0:T(8,128)(2,1)S(1)} %copy-done, bf16[4608,1152]{1,0:T(8,128)(2,1)} %param.6, f32[2048,1152]{1,0:T(8,128)} %fusion.8), kind=kOutput, calls=%fused_computation.10 | convolution fusion | flops 21766864896 | bytes 43646976 | tf_op jit(solution)/shard_map/dot_general | solution.py:10
  71.0 30.1 %convolution_convert_fusion = bf16[2048,4608]{1,0:T(8,128)(2,1)} fusion(bf16[2048,1152]{1,0:T(8,128)(2,1)S(1)} %fusion.7, bf16[1152,4608]{1,0:T(8,128)(2,1)} %param.7), kind=kOutput, calls=%fused_computation | convolution fusion | flops 21752709120 | bytes 34209792 | tf_op jit(solution)/shard_map/dot_general | solution.py:12
  101.1 0.0 all-reduce.2.cloned.1.call-update
  101.1 306.4 %all-reduce.2.cloned.1.call-done = bf16[2048,4608]{1,0:T(8,128)(2,1)} async-done(((bf16[2048,4608]{1,0:T(8,128)(2,1)}), bf16[2048,4608]{1,0:T(8,128)(2,1)}) %all-reduce.2.cloned.1.call-update) | async-done | bytes 18874384 | tf_op jit(solution)/shard_map/psum | solution.py:13
  407.5 16.5 %copy.6 = bf16[2048,4608]{1,0:T(8,128)(2,1)} copy(bf16[2048,4608]{1,0:T(8,128)(2,1)} %all-reduce.2.cloned.1.call-done) | data formatting | bytes 37748736
Async XLA Ops:
  6.5 401.0 %all-reduce.2.cloned.1.call-start = ((), (), s32[]{:S(2)}) async-start(), calls=%async_computation | async-start | bytes 37748736 | tf_op jit(solution)/shard_map/psum | solution.py:13
  6.5 32.0 %copy-start = (bf16[2048,4608]{1,0:T(8,128)(2,1)S(1)}, bf16[2048,4608]{1,0:T(8,128)(2,1)}, u32[]{:S(2)}) copy-start(bf16[2048,4608]{1,0:T(8,128)(2,1)} %param.4) | copy-start | bytes 56623108
Sparse Core Ops, SparseCore 0:
  101.2 306.2 all-reduce.1
where the time goes:
time: 431 us
  waiting for transfers between devices  306 us (71%)
  matrix products  94.5 us (22%)
  local copies, waits for them, and re-layouts  16.5 us (4%)
  between operations  13.4 us (3%)
    psum x1, waiting for transfers between devices, step(): return lax.psum(term, 'tp')  306 us
    dot_general x1, matrix products, step(): up = jnp.dot(x, w_up, preferred_element_type=jnp.float32)  32.4 us
    dot_general x1, matrix products, step(): gate = jnp.dot(x, w_gate, preferred_element_type=jnp.float32)  32 us
    dot_general x1, matrix products, step(): jnp.dot(hidden, w_down, preferred_element_type=jnp.float32)  30.1 us
    unnamed x3, local copies, waits for them, and re-layouts  16.5 us
  transfers between devices with their start and end apart: 1, of which 1 were waited for; matrix products, arithmetic and copies ran while one was open for 0% of the time, Pallas kernels for 0%

commit v1 on v0

v1 whole, which is shorter than its diff:
```python
import functools

import jax
import jax.numpy as jnp
from jax import lax
from jax.experimental import pallas as pl
from jax.experimental.pallas import tpu as pltpu
from jax.sharding import PartitionSpec as P

MESH = pl.DeviceIdType.MESH
F32, BF16 = jnp.float32, jnp.bfloat16

R = 128
LAST = 10

A_BLOCKS = (5, 5)
B_BLOCKS = (4, 4)


def kernel(dims, x_ref, wg_ref, wu_ref, wd_ref, y_ref,
           wgu, wdv, xb, hb, tb, stg, fin, rx1, rx2, rz1, rz2, rbz, rbm, rb1, rb2,
           wsem, xsem, ysem, ss, rs):
    rows, d, ff = dims
    n = rows // R
    half = d // 2
    nb = ff // 128
    W = tb.shape[0]
    me = lax.axis_index("tp")
    c = lax.rem(me, 2)
    z = lax.rem(me // 2, 4)
    yy = lax.rem(me // 8, 2)
    xx = me // 16

    def dev(px, py, pz, pc):
        return ((px * 2 + py) * 4 + pz) * 2 + pc

    xp = dev(1 - xx, yy, z, c)
    yp = dev(xx, 1 - yy, z, c)
    cp = dev(xx, yy, z, 1 - c)
    is_mid = (z == 1) | (z == 2)
    is_end = (z == 0) | (z == 3)
    m = z // 2
    om = dev(xx, yy, 3 - z, c)
    ez = dev(xx, yy, 3 * m, c)
    mz = dev(xx, yy, 1 + m, c)

    ids = {}

    def rc(name, k, src, dst, to):
        i = ids.setdefault(name, len(ids))
        return pltpu.make_async_remote_copy(
            src_ref=src, dst_ref=dst, send_sem=ss.at[i, k], recv_sem=rs.at[i, k],
            device_id={"tp": to}, device_id_type=MESH)

    def wcopy(i, part):
        src = (wg_ref, wu_ref)[part].at[:, pl.ds(i * 128, 128)]
        return pltpu.make_async_copy(src, wgu.at[i, :, pl.ds(part * 128, 128)], wsem.at[2 * i + part])

    def xcopy(k):
        return pltpu.make_async_copy(
            x_ref.at[pl.ds(pl.multiple_of(k * R, R), R), :], xb.at[lax.rem(k, 2)], xsem.at[lax.rem(k, 2)])

    def wd_own():
        return pltpu.make_async_copy(
            wd_ref.at[:, pl.ds(pl.multiple_of(c * half, 128), half)], wdv.at[pl.ds(0, ff)], wsem.at[2 * nb])

    def wd_part():
        return rc("wd", 0, wd_ref.at[:, pl.ds(pl.multiple_of((1 - c) * half, 128), half)],
                  wdv.at[pl.ds(ff, ff)], cp)

    xcopy(0).start()
    for i in range(nb):
        for part in range(2):
            wcopy(i, part).start()
    wd_own().start()

    bar = pltpu.get_barrier_semaphore()
    for peer in (xp, yp, cp):
        pl.semaphore_signal(bar, inc=1, device_id={"tp": peer}, device_id_type=MESH)

    @pl.when(is_mid)
    def _():
        pl.semaphore_signal(bar, inc=1, device_id={"tp": om}, device_id_type=MESH)
        pl.semaphore_signal(bar, inc=1, device_id={"tp": ez}, device_id_type=MESH)
        pl.semaphore_wait(bar, 5)

    @pl.when(is_end)
    def _():
        pl.semaphore_signal(bar, inc=1, device_id={"tp": mz}, device_id_type=MESH)
        pl.semaphore_wait(bar, 4)

    wd_part().start()

    A, B = [], []
    off = 0
    for j, blocks in enumerate(A_BLOCKS):
        ax = (xp, xx, yp, yy) if j == 0 else (yp, yy, xp, xx)
        A.append((f"A{j}", off, blocks * 128) + ax)
        off += blocks * 128
    boff = off
    for j, blocks in enumerate(B_BLOCKS):
        ax = (xp, xx, yp, yy) if j == 0 else (yp, yy, xp, xx)
        B.append((f"B{j}", off, blocks * 128) + ax)
        off += blocks * 128
    bw = off - boff
    R2, R4, R8 = R // 2, R // 4, R // 8
    bcols = pl.ds(boff, bw)

    def Y(k, row, nrows, o, w):
        return y_ref.at[pl.ds(pl.multiple_of(k * R + row, 16), nrows),
                        pl.ds(pl.multiple_of(c * half + o, 128), w)]

    def rows_at(start, size):
        return pl.ds(pl.multiple_of(start, 8), size)

    def a_msg(col, k, what):
        nm, o, w, p, a, q, b = col
        s = lax.rem(k, W)
        cols = pl.ds(o, w)
        q0 = a * R2 + b * R4
        key = nm + what
        if what == "xs":
            return rc(key, k, stg.at[s, pl.ds(0, R2), cols], rx1.at[k, :, cols], p)
        if what == "ys":
            return rc(key, k, stg.at[s, pl.ds(R2, R4), cols], rx2.at[k, :, cols], q)
        if what == "ze":
            return rc(key, k, stg.at[s, pl.ds(3 * R4, R4), cols], rz1.at[k, :, cols], mz)
        if what == "zm":
            return rc(key, k, stg.at[s, pl.ds(3 * R4, R8), cols], rz2.at[k, :, cols], om)
        if what == "gm":
            return rc(key, k, fin.at[s, :, cols], Y(k, q0 + m * R8, R8, o, w), om)
        reg = Y(k, q0, R4, o, w)
        if what == "ge":
            return rc(key, k, reg, reg, ez)
        if what == "gy":
            return rc(key, k, reg, reg, q)
        if what == "gx1":
            return rc(key, k, reg, reg, p)
        reg = Y(k, a * R2 + (1 - b) * R4, R4, o, w)
        assert what == "gx2"
        return rc(key, k, reg, reg, p)

    def b_msg(col, k, what):
        nm, o, w, p, a, q, b = col
        s = lax.rem(k, W)
        cols = pl.ds(o, w)
        lc = pl.ds(o - boff, w)
        key = nm + what
        if what == "xs":
            return rc(key, k, stg.at[s, pl.ds(R2, R4), cols], rb1.at[k, :, lc], p)
        if what == "ys":
            return rc(key, k, stg.at[s, pl.ds(3 * R4, R8), cols], rb2.at[k, :, lc], q)
        own = m * R2 + a * R4
        if what == "gy":
            return rc(key, k, fin.at[s, :, cols], Y(k, own + b * R8, R8, o, w), q)
        if what in ("gx", "gm1", "ge1"):
            reg = Y(k, own, R4, o, w)
            return rc(key, k, reg, reg, {"gx": p, "gm1": om, "ge1": ez}[what])
        if what in ("gm2", "ge2"):
            reg = Y(k, m * R2 + (1 - a) * R4, R4, o, w)
            return rc(key, k, reg, reg, {"gm2": om, "ge2": ez}[what])
        row = (1 - m) * R2 + {"ge3": a, "ge4": 1 - a}[what] * R4
        reg = Y(k, row, R4, o, w)
        return rc(key, k, reg, reg, ez)

    def bz_msg(k, what):
        s = lax.rem(k, W)
        if what == "ze":
            return rc("Bze", k, stg.at[s, :, bcols], rbz.at[k], mz)
        return rc("Bzm", k, stg.at[s, pl.ds(0, R2), bcols], rbm.at[k], om)

    def c_msg(k):
        reg = Y(k, 0, R, 0, half)
        return rc("cg", k, reg, reg, cp)

    def h_msg(k):
        sl = lax.rem(k, 4)
        return rc("h", k, hb.at[sl, :, pl.ds(0, ff)], hb.at[sl, :, pl.ds(ff, ff)], cp)

    def ylocal(col, j, k, row):
        nm, o, w = col[:3]
        s = lax.rem(k, W)
        return pltpu.make_async_copy(fin.at[s, :, pl.ds(o, w)], Y(k, row, R8, o, w), ysem.at[j, k])

    def a_fin_row(col):
        return col[4] * R2 + col[6] * R4 + m * R8

    def b_fin_row(col):
        return m * R2 + col[4] * R4 + col[6] * R8

    def h0(k):
        s = lax.rem(k, W)
        for col in A:
            nm, o, w, p, a, q, b = col
            cols = pl.ds(o, w)
            stg[s, pl.ds(0, R2), cols] = tb[s, rows_at((1 - a) * R2, R2), cols].astype(BF16)
            a_msg(col, k, "xs").start()

        @pl.when(is_end)
        def _():
            stg[s, :, bcols] = tb[s, :, bcols].astype(BF16)
            bz_msg(k, "ze").start()

    def h1(k):
        s = lax.rem(k, W)
        for col in A:
            nm, o, w, p, a, q, b = col
            cols = pl.ds(o, w)
            a_msg(col, k, "xs").wait_recv()
            snd, kp = (1 - b) * R4, b * R4
            stg[s, pl.ds(R2, R4), cols] = (
                tb[s, rows_at(a * R2 + snd, R4), cols]
                + rx1[k, rows_at(snd, R4), cols].astype(F32)).astype(BF16)
            a_msg(col, k, "ys").start()
            tb[s, rows_at(a * R2 + kp, R4), cols] += rx1[k, rows_at(kp, R4), cols].astype(F32)

        @pl.when(is_mid)
        def _():
            bz_msg(k, "ze").wait_recv()
            stg[s, pl.ds(0, R2), bcols] = (
                tb[s, rows_at((1 - m) * R2, R2), bcols]
                + rbz[k, rows_at((1 - m) * R2, R2), :].astype(F32)).astype(BF16)
            bz_msg(k, "zm").start()
            tb[s, rows_at(m * R2, R2), bcols] += rbz[k, rows_at(m * R2, R2), :].astype(F32)

    def h2(k):
        s = lax.rem(k, W)
        for col in A:
            nm, o, w, p, a, q, b = col
            cols = pl.ds(o, w)
            a_msg(col, k, "ys").wait_recv()
            q0 = rows_at(a * R2 + b * R4, R4)

            @pl.when(is_end)
            def _():
                stg[s, pl.ds(3 * R4, R4), cols] = (
                    tb[s, q0, cols] + rx2[k, :, cols].astype(F32)).astype(BF16)
                a_msg(col, k, "ze").start()

            @pl.when(is_mid)
            def _():
                tb[s, q0, cols] += rx2[k, :, cols].astype(F32)

        @pl.when(is_mid)
        def _():
            bz_msg(k, "zm").wait_recv()
            for col in B:
                nm, o, w, p, a, q, b = col
                cols, lc = pl.ds(o, w), pl.ds(o - boff, w)
                snd, kp = (1 - a) * R4, a * R4
                stg[s, pl.ds(R2, R4), cols] = (
                    tb[s, rows_at(m * R2 + snd, R4), cols]
                    + rbm[k, rows_at(snd, R4), lc].astype(F32)).astype(BF16)
                b_msg(col, k, "xs").start()
                tb[s, rows_at(m * R2 + kp, R4), cols] += rbm[k, rows_at(kp, R4), lc].astype(F32)

    def h3(k):
        s = lax.rem(k, W)

        @pl.when(is_mid)
        def _():
            for col in A:
                nm, o, w, p, a, q, b = col
                cols = pl.ds(o, w)
                a_msg(col, k, "ze").wait_recv()
                q0 = a * R2 + b * R4
                snd, kp = (1 - m) * R8, m * R8
                stg[s, pl.ds(3 * R4, R8), cols] = (
                    tb[s, rows_at(q0 + snd, R8), cols]
                    + rz1[k, rows_at(snd, R8), cols].astype(F32)).astype(BF16)
                a_msg(col, k, "zm").start()
                tb[s, rows_at(q0 + kp, R8), cols] += rz1[k, rows_at(kp, R8), cols].astype(F32)
            for col in B:
                nm, o, w, p, a, q, b = col
                cols, lc = pl.ds(o, w), pl.ds(o - boff, w)
                b_msg(col, k, "xs").wait_recv()
                q0 = m * R2 + a * R4
                snd, kp = (1 - b) * R8, b * R8
                stg[s, pl.ds(3 * R4, R8), cols] = (
                    tb[s, rows_at(q0 + snd, R8), cols]
                    + rb1[k, rows_at(snd, R8), lc].astype(F32)).astype(BF16)
                b_msg(col, k, "ys").start()
                tb[s, rows_at(q0 + kp, R8), cols] += rb1[k, rows_at(kp, R8), lc].astype(F32)

    def h4(k):
        s = lax.rem(k, W)

        @pl.when(is_mid)
        def _():
            for j, col in enumerate(A):
                nm, o, w, p, a, q, b = col
                cols = pl.ds(o, w)
                a_msg(col, k, "zm").wait_recv()
                fin[s, :, cols] = (
                    tb[s, rows_at(a_fin_row(col), R8), cols] + rz2[k, :, cols].astype(F32)).astype(BF16)
                a_msg(col, k, "gm").start()
                ylocal(col, j, k, a_fin_row(col)).start()
            for j, col in enumerate(B):
                nm, o, w, p, a, q, b = col
                cols, lc = pl.ds(o, w), pl.ds(o - boff, w)
                b_msg(col, k, "ys").wait_recv()
                fin[s, :, cols] = (
                    tb[s, rows_at(b_fin_row(col), R8), cols] + rb2[k, :, lc].astype(F32)).astype(BF16)
                b_msg(col, k, "gy").start()
                ylocal(col, 2 + j, k, b_fin_row(col)).start()

    def h5(k):
        @pl.when(is_mid)
        def _():
            for j, col in enumerate(A):
                ylocal(col, j, k, a_fin_row(col)).wait()
                a_msg(col, k, "gm").wait_recv()
                for what in ("ge", "gy", "gx1"):
                    a_msg(col, k, what).start()
            for j, col in enumerate(B):
                ylocal(col, 2 + j, k, b_fin_row(col)).wait()
                b_msg(col, k, "gy").wait_recv()
                for what in ("gx", "gm1", "ge1"):
                    b_msg(col, k, what).start()
            for col in A:
                for what in ("xs", "ys", "zm", "gm"):
                    a_msg(col, k, what).wait_send()
            bz_msg(k, "zm").wait_send()
            for col in B:
                for what in ("xs", "ys", "gy"):
                    b_msg(col, k, what).wait_send()

        @pl.when(is_end)
        def _():
            for col in A:
                for what in ("xs", "ys", "ze"):
                    a_msg(col, k, what).wait_send()
            bz_msg(k, "ze").wait_send()

    def h6(k):
        @pl.when(is_mid)
        def _():
            for col in A:
                a_msg(col, k, "gy").wait_recv()
                a_msg(col, k, "gx2").start()
            for col in B:
                b_msg(col, k, "gx").wait_recv()
                b_msg(col, k, "gm2").start()
                b_msg(col, k, "ge2").start()

        @pl.when(is_end)
        def _():
            for col in A:
                a_msg(col, k, "ge").wait_recv()
                a_msg(col, k, "gy").start()
                a_msg(col, k, "gx1").start()

    def h7(k):
        @pl.when(is_mid)
        def _():
            for col in B:
                b_msg(col, k, "gm1").wait_recv()
                b_msg(col, k, "ge3").start()
                b_msg(col, k, "gm2").wait_recv()
                b_msg(col, k, "ge4").start()

        @pl.when(is_end)
        def _():
            for col in A:
                a_msg(col, k, "gy").wait_recv()
                a_msg(col, k, "gx2").start()

    def h8(k):
        for col in A:
            a_msg(col, k, "gx1").wait_recv()
            a_msg(col, k, "gx2").wait_recv()

        @pl.when(is_end)
        def _():
            for col in B:
                for what in ("ge1", "ge2", "ge3", "ge4"):
                    b_msg(col, k, what).wait_recv()
        c_msg(k).start()

    def h9(k):
        c_msg(k).wait()
        for col in A:
            for what in ("gy", "gx1", "gx2"):
                a_msg(col, k, what).wait_send()

        @pl.when(is_mid)
        def _():
            for col in A:
                a_msg(col, k, "ge").wait_send()
            for col in B:
                for what in ("gx", "gm1", "gm2", "ge1", "ge2", "ge3", "ge4"):
                    b_msg(col, k, what).wait_send()

    handlers = [h1, h2, h3, h4, h5, h6, h7, h8, h9]
    nh = len(handlers)

    def run(s, t):
        k = t - 1 - s

        @pl.when((k >= 0) & (k < n))
        def _():
            handlers[s - 1](k)

    def tick(t, carry):
        order = list(range(nh, 0, -1))
        for i in range(nb):
            take = order[i * nh // nb:(i + 1) * nh // nb]
            for s in take:
                run(s, t)

            @pl.when(t < n)
            def _(i=i):
                if i == 0:
                    xcopy(t).wait()

                    @pl.when(t + 1 < n)
                    def _():
                        xcopy(t + 1).start()

                @pl.when(t == 0)
                def _():
                    wcopy(i, 0).wait()
                    wcopy(i, 1).wait()
                gu = jnp.dot(xb[lax.rem(t, 2)], wgu[i], preferred_element_type=F32)
                hb[lax.rem(t, 4), :, pl.ds(i * 128, 128)] = (
                    jax.nn.gelu(gu[:, :128]) * gu[:, 128:]).astype(BF16)

        @pl.when(t < n)
        def _():
            h_msg(t).start()

        @pl.when((t >= 1) & (t <= n))
        def _():
            k = t - 1

            @pl.when(t == 1)
            def _():
                wd_own().wait()
                wd_part().wait()
            h_msg(k).wait()
            s = lax.rem(k, W)
            for j in range(half // 256):
                tb[s, :, pl.ds(j * 256, 256)] = jnp.dot(
                    hb[lax.rem(k, 4)], wdv[:, pl.ds(j * 256, 256)], preferred_element_type=F32)
            h0(k)
        return carry

    lax.fori_loop(0, n + 1 + nh, tick, 0)


def solution(mesh):
    def step(x, w_gate, w_up, w_down):
        rows, d = x.shape
        ff = w_gate.shape[1]
        n, half = rows // R, d // 2
        aw, bw = 128 * sum(A_BLOCKS), 128 * sum(B_BLOCKS)
        assert aw + bw == half
        anyspec = pl.BlockSpec(memory_space=pl.ANY)
        ntypes = 44
        W = 5
        return pl.pallas_call(
            functools.partial(kernel, (rows, d, ff)),
            out_shape=jax.ShapeDtypeStruct((rows, d), BF16),
            in_specs=[anyspec] * 4,
            out_specs=anyspec,
            scratch_shapes=[
                pltpu.VMEM((ff // 128, d, 256), BF16),
                pltpu.VMEM((2 * ff, half), BF16),
                pltpu.VMEM((2, R, d), BF16),
                pltpu.VMEM((4, R, 2 * ff), BF16),
                pltpu.VMEM((W, R, half), F32),
                pltpu.VMEM((W, R, half), BF16),
                pltpu.VMEM((W, R // 8, half), BF16),
                pltpu.VMEM((n, R // 2, aw), BF16),
                pltpu.VMEM((n, R // 4, aw), BF16),
                pltpu.VMEM((n, R // 4, aw), BF16),
                pltpu.VMEM((n, R // 8, aw), BF16),
                pltpu.VMEM((n, R, bw), BF16),
                pltpu.VMEM((n, R // 2, bw), BF16),
                pltpu.VMEM((n, R // 4, bw), BF16),
                pltpu.VMEM((n, R // 8, bw), BF16),
                pltpu.SemaphoreType.DMA((2 * (ff // 128) + 1,)),
                pltpu.SemaphoreType.DMA((2,)),
                pltpu.SemaphoreType.DMA((4, n)),
                pltpu.SemaphoreType.DMA((ntypes, n)),
                pltpu.SemaphoreType.DMA((ntypes, n)),
            ],
            compiler_params=pltpu.CompilerParams(
                collective_id=0, has_side_effects=True, vmem_limit_bytes=67043328),
        )(x, w_gate, w_up, w_down)

    return jax.shard_map(
        step,
        mesh=mesh,
        in_specs=(P("dp", None), P(None, "tp"), P(None, "tp"), P("tp", None)),
        out_specs=P("dp", None),
        check_vma=False,
    )
```

time: 431 us -> 211 us (0.49)
  waiting for transfers between devices: 306 us -> 0 us
  Pallas kernels: 0 us -> 194 us
  matrix products: 94.5 us -> 0 us
  between operations: 13.4 us -> 0.01 us
    psum x1 -> x0, waiting for transfers between devices: 306 us -> none  [step(): return lax.psum(term, 'tp')]
    pallas_call x0 -> x1, Pallas kernels: none -> 194 us  [step(): pl.pallas_call(functools.partial(kernel, (rows, d, ff)), out_shape=jax.Sh...]
    dot_general x3 -> x0, matrix products: 94.5 us -> none  [the longest x1 32.4 us: step(): up = jnp.dot(x, w_up, preferred_element_type=jnp.float32)]
    unnamed x3 -> x1, local copies, waits for them, and re-layouts: 16.5 us -> 16.5 us
  transfers between devices with their start and end apart: 1 -> 0, of which waited for: 1 -> 0; matrix products, arithmetic and copies ran while one was open for 0% -> 0% of each run, Pallas kernels for 0% -> 0%
where the time goes in v1:
time: 211 us
  Pallas kernels  194 us (92%)
  local copies, waits for them, and re-layouts  16.5 us (8%)
    pallas_call x1, Pallas kernels, step(): pl.pallas_call(functools.partial(kernel, (rows, d, ff)), out_shape=jax.Sh...  194 us
    unnamed x1, local copies, waits for them, and re-layouts  16.5 us

profile of v1, /device:TPU:0, one launch (start us, length us, event | category | flops | bytes accessed | tf_op | source)
XLA Modules:
  0.0 210.7 jit_solution(5222698496348326674)
XLA Ops:
  0.0 194.2 %shard_map.46 = bf16[2048,4608]{1,0:T(8,128)(2,1)} custom-call(bf16[2048,4608]{1,0:T(8,128)(2,1)} %x_ref.1, bf16[4608,1152]{1,0:T(8,128)(2,1)} %wg_ref.1, bf16[4608,1152]{1,0:T(8,128)(2,1)} %wu_ref.1, bf16[1152,4608]{1,0:T(8,128)(2,1)} %wd_ref.1), custom_call_target="tpu_custom_call" | custom-call | tf_op jit(solution)/shard_map/pallas_call | solution.py:461
  194.2 16.5 %copy.6 = bf16[2048,4608]{1,0:T(8,128)(2,1)} copy(bf16[2048,4608]{1,0:T(8,128)(2,1)} %shard_map.46) | data formatting | bytes 37748736

commit v2 on v1

--- a/solution.py
+++ b/solution.py
@@ -11,15 +11,16 @@
 F32, BF16 = jnp.float32, jnp.bfloat16
 
 R = 128
-LAST = 10
-
-A_BLOCKS = (5, 5)
-B_BLOCKS = (4, 4)
-
-
-def kernel(dims, x_ref, wg_ref, wu_ref, wd_ref, y_ref,
-           wgu, wdv, xb, hb, tb, stg, fin, rx1, rx2, rz1, rz2, rbz, rbm, rb1, rb2,
-           wsem, xsem, ysem, ss, rs):
+
+VMEM_LIMIT = 37 * 2**20
+
+A_BLOCKS = (7, 7)
+B_BLOCKS = (2, 2)
+
+
+def kernel(dims, x_ref, wg_ref, wu_ref, wd_ref, y_ref, wgu,
+           wdv, xb, hb, tb, stg, fin, rx1, rx2, rz1, rz2, rbz, rbm, rb1, rb2,
+           wsem, xsem, ysem, vsem, ss, rs):
     rows, d, ff = dims
     n = rows // R
     half = d // 2
@@ -54,7 +55,7 @@
 
     def wcopy(i, part):
         src = (wg_ref, wu_ref)[part].at[:, pl.ds(i * 128, 128)]
-        return pltpu.make_async_copy(src, wgu.at[i, :, pl.ds(part * 128, 128)], wsem.at[2 * i + part])
+        return pltpu.make_async_copy(src, wgu.at[pl.ds(i * d, d), pl.ds(part * 128, 128)], wsem.at[2 * i + part])
 
     def xcopy(k):
         return pltpu.make_async_copy(
@@ -111,7 +112,7 @@
                         pl.ds(pl.multiple_of(c * half + o, 128), w)]
 
     def rows_at(start, size):
-        return pl.ds(pl.multiple_of(start, 8), size)
+        return pl.ds(pl.multiple_of(start, 16), size)
 
     def a_msg(col, k, what):
         nm, o, w, p, a, q, b = col
@@ -177,6 +178,12 @@
         sl = lax.rem(k, 4)
         return rc("h", k, hb.at[sl, :, pl.ds(0, ff)], hb.at[sl, :, pl.ds(ff, ff)], cp)
 
+    def to_vmem(k, j):
+        r0 = pl.multiple_of(k * R, R)
+        return pltpu.make_async_copy(
+            y_ref.at[pl.ds(r0, R), pl.ds(j * 256, 256)],
+            wgu.at[pl.ds(pl.multiple_of(j * rows + r0, R), R), :], vsem.at[k, j])
+
     def ylocal(col, j, k, row):
         nm, o, w = col[:3]
         s = lax.rem(k, W)
@@ -394,58 +401,95 @@
     handlers = [h1, h2, h3, h4, h5, h6, h7, h8, h9]
     nh = len(handlers)
 
-    def run(s, t):
-        k = t - 1 - s
-
-        @pl.when((k >= 0) & (k < n))
-        def _():
-            handlers[s - 1](k)
+    def run(t, *stages):
+        for s in stages:
+            k = t - 1 - s
+
+            @pl.when((k >= 0) & (k < n))
+            def _(s=s, k=k):
+                handlers[s - 1](k)
+
+    def gateup(t, lo, hi, first):
+        for i in range(lo, hi):
+            if first:
+                wcopy(i, 0).wait()
+                wcopy(i, 1).wait()
+            gu = jnp.dot(xb[lax.rem(t, 2)], wgu[pl.ds(i * d, d), :], preferred_element_type=F32)
+            hb[lax.rem(t, 4), :, pl.ds(i * 128, 128)] = (
+                jax.nn.gelu(gu[:, :128]) * gu[:, 128:]).astype(BF16)
+
+    def down(k):
+        h_msg(k).wait()
+        s = lax.rem(k, W)
+        for j in range(half // 256):
+            tb[s, :, pl.ds(j * 256, 256)] = jnp.dot(
+                hb[lax.rem(k, 4)], wdv[:, pl.ds(j * 256, 256)], preferred_element_type=F32)
+
+    xcopy(0).wait()
+    xcopy(1).start()
+    gateup(0, 0, nb, True)
+    h_msg(0).start()
+    wd_own().wait()
+    wd_part().wait()
 
     def tick(t, carry):
-        order = list(range(nh, 0, -1))
-        for i in range(nb):
-            take = order[i * nh // nb:(i + 1) * nh // nb]
-            for s in take:
-                run(s, t)
-
-            @pl.when(t < n)
-            def _(i=i):
-                if i == 0:
-                    xcopy(t).wait()
-
-                    @pl.when(t + 1 < n)
-                    def _():
-                        xcopy(t + 1).start()
-
-                @pl.when(t == 0)
-                def _():
-                    wcopy(i, 0).wait()
-                    wcopy(i, 1).wait()
-                gu = jnp.dot(xb[lax.rem(t, 2)], wgu[i], preferred_element_type=F32)
-                hb[lax.rem(t, 4), :, pl.ds(i * 128, 128)] = (
-                    jax.nn.gelu(gu[:, :128]) * gu[:, 128:]).astype(BF16)
-
-        @pl.when(t < n)
-        def _():
-            h_msg(t).start()
-
-        @pl.when((t >= 1) & (t <= n))
-        def _():
-            k = t - 1
-
-            @pl.when(t == 1)
-            def _():
-                wd_own().wait()
-                wd_part().wait()
-            h_msg(k).wait()
-            s = lax.rem(k, W)
-            for j in range(half // 256):
-                tb[s, :, pl.ds(j * 256, 256)] = jnp.dot(
-                    hb[lax.rem(k, 4)], wdv[:, pl.ds(j * 256, 256)], preferred_element_type=F32)
-            h0(k)
+        run(t, 9, 8, 7, 6)
+        xcopy(t).wait()
+
+        @pl.when(t + 1 < n)
+        def _():
+            xcopy(t + 1).start()
+        gateup(t, 0, 5, False)
+        run(t, 5, 4, 3)
+        gateup(t, 5, nb, False)
+        h_msg(t).start()
+        down(t - 1)
+        run(t, 2, 1)
+        h0(t - 1)
         return carry
 
-    lax.fori_loop(0, n + 1 + nh, tick, 0)
+    lax.fori_loop(1, n, tick, 0)
+    down(n - 1)
+    run(n, 9, 8, 7, 6, 5, 4, 3, 2, 1)
+    h0(n - 1)
+
+    def fetch(k):
+        for j in range(d // 256):
+            to_vmem(k, j).start()
+
+    early = n - nh
+
+    def fetch_early(k, carry):
+        fetch(k)
+        return carry
+
+    lax.fori_loop(0, early, fetch_early, 0)
+
+    def drain(t, carry):
+        run(t, 9, 8, 7, 6, 5, 4, 3, 2, 1)
+        fetch(t - 1 - nh)
+        return carry
+
+    lax.fori_loop(n + 1, n + 1 + nh, drain, 0)
+
+    def fetched(k, carry):
+        for j in range(d // 256):
+            to_vmem(k, j).wait()
+        return carry
+
+    lax.fori_loop(0, n, fetched, 0)
+
+
+def store_kernel(v_ref, o_ref, sem):
+    rows, d = o_ref.shape
+    copies = [
+        pltpu.make_async_copy(
+            v_ref.at[pl.ds(j * rows, rows), :], o_ref.at[:, pl.ds(j * 256, 256)], sem.at[j])
+        for j in range(d // 256)]
+    for c in copies:
+        c.start()
+    for c in copies:
+        c.wait()
 
 
 def solution(mesh):
@@ -458,13 +502,13 @@
         anyspec = pl.BlockSpec(memory_space=pl.ANY)
         ntypes = 44
         W = 5
-        return pl.pallas_call(
+        _, v = pl.pallas_call(
             functools.partial(kernel, (rows, d, ff)),
-            out_shape=jax.ShapeDtypeStruct((rows, d), BF16),
+            out_shape=[jax.ShapeDtypeStruct((rows, d), BF16),
+                       pltpu.VMEM((ff // 128 * d, 256), BF16)],
             in_specs=[anyspec] * 4,
-            out_specs=anyspec,
+            out_specs=[anyspec, pl.BlockSpec(memory_space=pltpu.VMEM)],
             scratch_shapes=[
-                pltpu.VMEM((ff // 128, d, 256), BF16),
                 pltpu.VMEM((2 * ff, half), BF16),
                 pltpu.VMEM((2, R, d), BF16),
                 pltpu.VMEM((4, R, 2 * ff), BF16),
@@ -482,12 +526,21 @@
                 pltpu.SemaphoreType.DMA((2 * (ff // 128) + 1,)),
                 pltpu.SemaphoreType.DMA((2,)),
                 pltpu.SemaphoreType.DMA((4, n)),
+                pltpu.SemaphoreType.DMA((n, d // 256)),
                 pltpu.SemaphoreType.DMA((ntypes, n)),
                 pltpu.SemaphoreType.DMA((ntypes, n)),
             ],
             compiler_params=pltpu.CompilerParams(
-                collective_id=0, has_side_effects=True, vmem_limit_bytes=67043328),
+                collective_id=0, has_side_effects=True, vmem_limit_bytes=VMEM_LIMIT),
         )(x, w_gate, w_up, w_down)
+        return pl.pallas_call(
+            store_kernel,
+            out_shape=jax.ShapeDtypeStruct((rows, d), BF16),
+            in_specs=[pl.BlockSpec(memory_space=pltpu.VMEM)],
+            out_specs=anyspec,
+            scratch_shapes=[pltpu.SemaphoreType.DMA((d // 256,))],
+            compiler_params=pltpu.CompilerParams(vmem_limit_bytes=2**20),
+        )(v)
 
     return jax.shard_map(
         step,

time: 211 us -> 202 us (0.957)
  local copies, waits for them, and re-layouts: 16.5 us -> 0 us
  Pallas kernels: 194 us -> 201 us
    unnamed x1 -> x0, local copies, waits for them, and re-layouts: 16.5 us -> none
    pallas_call x1 -> x2, Pallas kernels: 194 us -> 201 us  [the longest x1 195 us: step(): pl.pallas_call(functools.partial(kernel, (rows, d, ff)), out_shape=[jax.S...]
where the time goes in v2:
time: 202 us
  Pallas kernels  201 us (100%)
    pallas_call x1, Pallas kernels, step(): pl.pallas_call(functools.partial(kernel, (rows, d, ff)), out_shape=[jax.S...  195 us
    pallas_call x1, Pallas kernels, step(): pl.pallas_call(store_kernel, out_shape=jax.ShapeDtypeStruct((rows, d), BF...  6.61 us

profile of v2, /device:TPU:0, one launch (start us, length us, event | category | flops | bytes accessed | tf_op | source)
XLA Modules:
  0.0 201.5 jit_solution(10418812120280490884)
XLA Ops:
  0.0 194.8 %shard_map.46 = (bf16[2048,4608]{1,0:T(8,128)(2,1)}, bf16[41472,256]{1,0:T(8,128)(2,1)S(1)}) custom-call(bf16[2048,4608]{1,0:T(8,128)(2,1)} %x_ref.1, bf16[4608,1152]{1,0:T(8,128)(2,1)} %wg_ref.1, bf16[4608,1152]{1,0:T(8,128)(2,1)} %wu_ref.1, bf16[1152,4608]{1,0:T(8,128)(2,1)} %wd_ref.1), custom_call_target="tpu_custom_call" | custom-call | tf_op jit(solution)/shard_map/pallas_call | solution.py:505
  194.8 6.6 %shard_map.47 = bf16[2048,4608]{1,0:T(8,128)(2,1)} custom-call(bf16[41472,256]{1,0:T(8,128)(2,1)S(1)} %get-tuple-element.6.v_ref), custom_call_target="tpu_custom_call" | custom-call | tf_op jit(solution)/shard_map/pallas_call | solution.py:536
